TPU v7x, 32 devices: a whole 2x2x4 slice. The times are simulated.
32 devices in a mesh: tile: 8 (over z, y), lev: 4 (over x, core).
Axes of the slice: x: 2, y: 2, z: 4, core: 2. Of those that a mesh axis runs over, the one named last changes fastest.
Arguments:
- ensemble: bfloat16 [80, 32, 4096], P(None, 'lev', 'tile')
- pair_first: int32 [32768], P('tile'), may hold values from 0 to 511
- pair_second: int32 [32768], P('tile'), may hold values from 0 to 1023
- pair_bin: int32 [32768], P('tile'), may hold values from 0 to 63, as said below
Outputs:
- level_variance: float32 [32], P('lev')
- bin_corr: float32 [32, 64], P('lev', 'tile')
- bin_avg: float32 [64], P('tile')
Inputs may be any that keep to these rules, and one draw needn't show every extreme that they name: `pair_bin`: some bins receive no pair; which ones changes with the draw.
All inputs are finite; a program needn't handle non-finite values.
Results may differ from a plain program's by a relative error of at most 0.0017.
Values may be sent and summed in bfloat16 or wider, within the bound.
A program may use at most 64 MiB of HBM per device.

v0:
```python
import functools

import jax
import jax.numpy as jnp
from jax import lax
from jax.experimental import pallas as pl
from jax.experimental.pallas import tpu as pltpu
from jax.sharding import PartitionSpec as P

BIN_DEV = 8
LANES = 128
PAIR_CHUNK = 512
HALO_CHUNKS = 2


def pieces3(x):
    a = x.astype(jnp.bfloat16).astype(jnp.float32)
    r = x - a
    b = r.astype(jnp.bfloat16).astype(jnp.float32)
    return a, b, r - b


def onehot(rows, base, count):
    ids = lax.broadcasted_iota(jnp.int32, (count, LANES), 0) + base
    parts = [jnp.where(ids == r, 1.0, 0.0) for r in rows]
    return jnp.concatenate(parts, axis=1).astype(jnp.bfloat16)


def perturb(raw, out, squares, width):
    members, lev = raw.shape[0], raw.shape[1]
    rows = members * lev
    for c in range(0, width, LANES):
        cs = pl.ds(c, LANES)
        x = raw[:, :, cs].astype(jnp.float32)
        mean = jnp.sum(x, axis=0) / members
        pert = (x - mean[None]).astype(jnp.bfloat16).astype(jnp.float32)
        sq = jnp.sum(pert * pert, axis=0)
        out[pl.ds(0, rows), cs] = pert.reshape(rows, LANES).astype(jnp.bfloat16)
        inv = 1.0 / jnp.sqrt(sq / (members - 1) + 1e-06)
        hi = inv.astype(jnp.bfloat16).astype(jnp.float32)
        out[pl.ds(rows, 2 * lev), cs] = jnp.concatenate([hi, inv - hi], axis=0).astype(jnp.bfloat16)
        if squares is not None:
            squares[:, cs] = sq


def spread_lanes(x, lev):
    lane = lax.broadcasted_iota(jnp.int32, x.shape, 1)
    s = x + pltpu.roll(x, LANES - lev, 1) + pltpu.roll(x, LANES - 2 * lev, 1)
    s = jnp.where(lane < lev, s, 0.0)
    width = lev
    while width < BIN_DEV * lev:
        s = s + pltpu.roll(s, width, 1)
        width *= 2
    return s


def kernel(
    ntile, nlev, ens, first_in, second_in, bin_in, packed,
    raw, halo, first, second, bins, own, nxt, squares, left_buf, cov_buf, ia_buf, ib_buf,
    bin_hot, parts_buf, bacc, sq_buf, sbuf, rbuf,
    load_sem, halo_send, halo_recv, x_send, x_recv, ready,
):
    members, lev, cols = ens.shape
    rows = members * lev
    half = cols // HALO_CHUNKS
    npairs = bin_hot.shape[1]
    total_bins = BIN_DEV * ntile
    chunks = left_buf.shape[0]
    groups = PAIR_CHUNK // LANES
    me = lax.axis_index("tile")
    my_lev = lax.axis_index("lev")

    barrier = pltpu.get_barrier_semaphore()
    for d in range(1, ntile):
        pl.semaphore_signal(
            barrier, inc=1, device_id=(lax.rem(me + d, ntile), my_lev),
            device_id_type=pl.DeviceIdType.MESH,
        )
    for d in range(1, nlev):
        pl.semaphore_signal(
            barrier, inc=1, device_id=(me, lax.rem(my_lev + d, nlev)),
            device_id_type=pl.DeviceIdType.MESH,
        )
    loads = [
        pltpu.make_async_copy(s, d, load_sem.at[i])
        for i, (s, d) in enumerate(
            ((ens, raw), (first_in, first), (second_in, second), (bin_in, bins))
        )
    ]
    for c in loads:
        c.start()
    loads[0].wait()
    pl.semaphore_wait(barrier, ntile - 1 + nlev - 1)
    prev = lax.rem(me + ntile - 1, ntile)
    halos = [
        pltpu.make_async_remote_copy(
            src_ref=raw.at[:, :, pl.ds(h * half, half)],
            dst_ref=halo.at[h],
            send_sem=halo_send.at[h],
            recv_sem=halo_recv.at[h],
            device_id=(prev, my_lev),
            device_id_type=pl.DeviceIdType.MESH,
        )
        for h in range(HALO_CHUNKS)
    ]
    for c in halos:
        c.start()
    for d in range(1, nlev):
        pl.semaphore_signal(
            ready, inc=1, device_id=(me, lax.rem(my_lev + d, nlev)),
            device_id_type=pl.DeviceIdType.MESH,
        )
    for c in loads[1:]:
        c.wait()

    perturb(raw, own, squares, cols)

    def index_rows(ref, j):
        return [ref[pl.ds(j * groups + i, 1), :] for i in range(groups)]

    def product(a, b):
        return jnp.sum((a * b).reshape(members, lev, PAIR_CHUNK), axis=0)

    def own_step(j, carry):
        x = own[...]
        left = jnp.dot(x, onehot(index_rows(first, j), 0, cols), preferred_element_type=jnp.float32)
        left_buf[j] = left[:rows]
        right = jnp.dot(x, onehot(index_rows(second, j), 0, cols), preferred_element_type=jnp.float32)
        cov_buf[j] = product(left_buf[j], right[:rows])
        ia_buf[j] = left[rows:rows + lev] + left[rows + lev:]
        ib_buf[j] = right[rows:rows + lev] + right[rows + lev:]
        return carry

    lax.fori_loop(0, chunks, own_step, 0)
    def bin_step(j, carry):
        cs = pl.ds(pl.multiple_of(j * PAIR_CHUNK, PAIR_CHUNK), PAIR_CHUNK)
        bin_hot[:, cs] = onehot(index_rows(bins, j), 0, total_bins)
        return carry

    lax.fori_loop(0, chunks, bin_step, 0)
    parts_buf[...] = jnp.concatenate(
        [jnp.zeros((BIN_DEV * lev, npairs), jnp.float32), jnp.ones((LANES - BIN_DEV * lev, npairs), jnp.float32)], axis=0
    ).astype(jnp.bfloat16)
    sq_parts = jnp.concatenate(
        [*pieces3(squares[...]), jnp.zeros((LANES - 3 * lev, cols), jnp.float32)], axis=0
    ).astype(jnp.bfloat16)
    sq_row = lax.dot_general(
        jnp.ones((16, cols), jnp.bfloat16), sq_parts, (((1,), (1,)), ((), ())),
        preferred_element_type=jnp.float32,
    )[:BIN_DEV]
    sq_buf[...] = spread_lanes(sq_row, lev)
    pl.semaphore_wait(ready, nlev - 1)

    for h in range(HALO_CHUNKS):
        halos[h].wait_recv()
        perturb(halo.at[h], nxt.at[h], None, half)

        def next_step(j, carry):
            oh = onehot(index_rows(second, j), cols + h * half, half)
            right = jnp.dot(nxt[h], oh, preferred_element_type=jnp.float32)
            cov = cov_buf[j] + product(left_buf[j], right[:rows])
            ib = ib_buf[j] + right[rows:rows + lev] + right[rows + lev:]
            if h < HALO_CHUNKS - 1:
                cov_buf[j] = cov
                ib_buf[j] = ib
            else:
                corr = cov * ia_buf[j] * ib / (members - 1)
                parts = jnp.concatenate(
                    [*pieces3(corr), jnp.zeros_like(corr)], axis=0
                ).astype(jnp.bfloat16)
                parts_buf[pl.ds(0, 4 * lev), pl.ds(pl.multiple_of(j * PAIR_CHUNK, PAIR_CHUNK), PAIR_CHUNK)] = parts
            return carry

        lax.fori_loop(0, chunks, next_step, 0, unroll=8)

    bacc[...] = lax.dot_general(
        bin_hot[...], parts_buf[...], (((1,), (1,)), ((), ())), preferred_element_type=jnp.float32
    )
    half_lanes = BIN_DEV * lev
    wide_lane = lax.broadcasted_iota(jnp.int32, (total_bins, LANES), 1)
    wide = jnp.where(wide_lane < half_lanes, spread_lanes(bacc[...], lev), bacc[...])
    lane = lax.broadcasted_iota(jnp.int32, (BIN_DEV, LANES), 1)
    bin_row = lax.broadcasted_iota(jnp.int32, (BIN_DEV, LANES), 0)
    pick = (lax.rem(lane, half_lanes) // lev == bin_row).astype(jnp.float32)
    for t in range(ntile):
        block = wide[t * BIN_DEV:(t + 1) * BIN_DEV] * pick
        sbuf[t, 0:1, :] = jnp.sum(block, axis=0, keepdims=True)
        sbuf[t, 1:2, :] = sq_buf[0:1, :]
    mine = my_lev * ntile + me
    rbuf[mine] = sbuf[me]

    def x_copy(d):
        dl, dt = d // ntile, d % ntile
        peer_t = lax.rem(me + dt, ntile)
        peer_l = lax.rem(my_lev + dl, nlev)
        return pltpu.make_async_remote_copy(
            src_ref=sbuf.at[peer_t], dst_ref=rbuf.at[mine],
            send_sem=x_send.at[d], recv_sem=x_recv.at[mine],
            device_id=(peer_t, peer_l), device_id_type=pl.DeviceIdType.MESH,
        )

    def x_start(d, carry):
        x_copy(d).start()
        return carry

    def x_wait_send(d, carry):
        x_copy(d).wait_send()
        return carry

    def x_wait(d, carry):
        src = lax.rem(my_lev + d // ntile, nlev) * ntile + lax.rem(me + d % ntile, ntile)
        pltpu.make_async_copy(rbuf.at[src], rbuf.at[src], x_recv.at[src]).wait()
        return carry

    everyone = ntile * nlev
    small = everyone <= 64
    lax.fori_loop(1, everyone, x_start, 0, unroll=small)
    lax.fori_loop(1, everyone, x_wait, 0, unroll=small)
    num = jnp.zeros((1, LANES), jnp.float32)
    den = num
    own_lv = num
    own_bc = num
    for v in range(nlev):
        tot = rbuf[v * ntile]
        for t in range(1, ntile):
            tot = tot + rbuf[v * ntile + t]
        sums, lv = tot[0:1], tot[1:2] / ((members - 1) * cols * ntile)
        bc = sums / jnp.maximum(pltpu.roll(sums, LANES - half_lanes, 1), 1.0)
        num = num + lv * bc
        den = den + lv
        own_lv = jnp.where(my_lev == v, lv, own_lv)
        own_bc = jnp.where(my_lev == v, bc, own_bc)
    for i, row in enumerate((own_lv, own_bc, num, den)):
        packed[i:i + 1, :] = row

    for c in halos:
        c.wait_send()
    lax.fori_loop(1, everyone, x_wait_send, 0, unroll=small)


def unpack(packed, lv_out, corr_out, avg_out):
    lev = corr_out.shape[0]
    lane = lax.broadcasted_iota(jnp.int32, (BIN_DEV, LANES), 1)
    bin_row = lax.broadcasted_iota(jnp.int32, (BIN_DEV, LANES), 0)

    def by_bin(row):
        x = jnp.where(lane // lev == bin_row, row, 0.0)
        return jnp.sum(jnp.transpose(x).reshape(LANES // lev, lev, BIN_DEV), axis=0)

    lv_out[...] = packed[0:1, :lev]
    corr_out[...] = by_bin(packed[1:2, :])
    num = jnp.sum(by_bin(packed[2:3, :]), axis=0, keepdims=True)
    den = jnp.sum(by_bin(packed[3:4, :]), axis=0, keepdims=True)
    avg_out[...] = num / den


def local(ntile, nlev, ensemble, pair_first, pair_second, pair_bin):
    members, lev, cols = ensemble.shape
    npairs = pair_first.shape[0]
    rows = members * lev
    half = cols // HALO_CHUNKS
    chunks = npairs // PAIR_CHUNK
    total_bins = BIN_DEV * ntile
    f32, bf16 = jnp.float32, jnp.bfloat16
    idx = [x.reshape(npairs // LANES, LANES) for x in (pair_first, pair_second, pair_bin)]
    vmem = pl.BlockSpec(memory_space=pltpu.VMEM)
    hbm = pl.BlockSpec(memory_space=pl.ANY)
    packed = pl.pallas_call(
        functools.partial(kernel, ntile, nlev),
        out_shape=jax.ShapeDtypeStruct((8, LANES), f32),
        in_specs=[hbm] * 4,
        out_specs=vmem,
        scratch_shapes=[
            pltpu.VMEM((members, lev, cols), bf16),
            pltpu.VMEM((HALO_CHUNKS, members, lev, half), bf16),
            *[pltpu.VMEM((npairs // LANES, LANES), jnp.int32)] * 3,
            pltpu.VMEM((rows + 2 * lev, cols), bf16),
            pltpu.VMEM((HALO_CHUNKS, rows + 2 * lev, half), bf16),
            pltpu.VMEM((lev, cols), f32),
            pltpu.VMEM((chunks, rows, PAIR_CHUNK), f32),
            *[pltpu.VMEM((chunks, lev, PAIR_CHUNK), f32)] * 3,
            pltpu.VMEM((total_bins, npairs), bf16),
            pltpu.VMEM((LANES, npairs), bf16),
            pltpu.VMEM((total_bins, LANES), f32),
            pltpu.VMEM((BIN_DEV, LANES), f32),
            pltpu.VMEM((ntile, 2, LANES), f32),
            pltpu.VMEM((nlev * ntile, 2, LANES), f32),
            pltpu.SemaphoreType.DMA((4,)),
            pltpu.SemaphoreType.DMA((HALO_CHUNKS,)),
            pltpu.SemaphoreType.DMA((HALO_CHUNKS,)),
            pltpu.SemaphoreType.DMA((nlev * ntile,)),
            pltpu.SemaphoreType.DMA((nlev * ntile,)),
            pltpu.SemaphoreType.REGULAR,
        ],
        compiler_params=pltpu.CompilerParams(
            collective_id=0, has_side_effects=True, vmem_limit_bytes=60 * 1024 * 1024
        ),
        name="binned_corr",
    )(ensemble, *idx)
    lv, corr, avg = pl.pallas_call(
        unpack,
        out_shape=(
            jax.ShapeDtypeStruct((1, lev), f32),
            jax.ShapeDtypeStruct((lev, BIN_DEV), f32),
            jax.ShapeDtypeStruct((1, BIN_DEV), f32),
        ),
        in_specs=[vmem],
        out_specs=(vmem, vmem, vmem),
        name="unpack",
    )(packed)
    return lv.reshape(lev), corr, avg.reshape(BIN_DEV)


def solution(mesh):
    in_specs = (P(None, "lev", "tile"), P("tile"), P("tile"), P("tile"))
    out_specs = (P("lev"), P("lev", "tile"), P("tile"))
    body = functools.partial(local, mesh.shape["tile"], mesh.shape["lev"])
    return jax.shard_map(body, mesh=mesh, in_specs=in_specs, out_specs=out_specs, check_vma=False)
```

profile of v0, /device:TPU:0, one launch (start us, length us, event | category | flops | bytes accessed | tf_op | source)
XLA Modules:
  0.0 33.7 jit_solution(8867087564475353142)
XLA Ops:
  0.6 31.7 %binned_corr.1.packed = f32[8,128]{1,0:T(8,128)} custom-call(bf16[80,8,512]{2,1,0:T(8,128)(2,1)} %ens.1, s32[32,128]{1,0:T(8,128)} %bitcast.5, s32[32,128]{1,0:T(8,128)} %bitcast.6, s32[32,128]{1,0:T(8,128)} %bitcast.7), custom_call_target="tpu_custom_call" | custom-call | tf_op jit(solution)/shard_map/binned_corr/pallas_call | solution.py:268
  32.4 1.4 %unpack.1 = (f32[1,8]{1,0:T(1,128)}, f32[8,8]{1,0:T(8,128)}, f32[1,8]{1,0:T(1,128)}) custom-call(f32[8,128]{1,0:T(8,128)} %binned_corr.1.packed), custom_call_target="tpu_custom_call" | custom-call | tf_op jit(solution)/shard_map/unpack/pallas_call | solution.py:300
where the time goes:
time: 33.9 us; the launch traced here: 33.7 us
  Pallas kernels  33.1 us (98%)
  between operations  0.64 us (2%)
    pallas_call x1, Pallas kernels, local(): pl.pallas_call(functools.partial(kernel, ntile, nlev), out_shape=jax.Shap...  31.7 us
    pallas_call x1, Pallas kernels, local(): pl.pallas_call(unpack, out_shape=(jax.ShapeDtypeStruct((1, lev), f32), ja...  1.37 us

commit v1 on v0

--- a/solution.py
+++ b/solution.py
@@ -293,7 +293,7 @@
             pltpu.SemaphoreType.REGULAR,
         ],
         compiler_params=pltpu.CompilerParams(
-            collective_id=0, has_side_effects=True, vmem_limit_bytes=60 * 1024 * 1024
+            collective_id=0, has_side_effects=True, vmem_limit_bytes=55220 * 1024
         ),
         name="binned_corr",
     )(ensemble, *idx)
@@ -306,6 +306,7 @@
         ),
         in_specs=[vmem],
         out_specs=(vmem, vmem, vmem),
+        compiler_params=pltpu.CompilerParams(vmem_limit_bytes=4 * 1024 * 1024),
         name="unpack",
     )(packed)
     return lv.reshape(lev), corr, avg.reshape(BIN_DEV)

time: 33.9 us -> 32.6 us (0.962)
  Pallas kernels: 33.1 us -> 31.8 us
    pallas_call x1, Pallas kernels: 1.37 us -> 0.7 us  [local(): pl.pallas_call(unpack, out_shape=(jax.ShapeDtypeStruct((1, lev), f32), ja...]
    pallas_call x1, Pallas kernels: 31.7 us -> 31.1 us  [local(): pl.pallas_call(functools.partial(kernel, ntile, nlev), out_shape=jax.Shap...]
where the time goes in v1:
time: 32.6 us; the launch traced here: 32.5 us
  Pallas kernels  31.8 us (98%)
  between operations  0.64 us (2%)
    pallas_call x1, Pallas kernels, local(): pl.pallas_call(functools.partial(kernel, ntile, nlev), out_shape=jax.Shap...  31.1 us
    pallas_call x1, Pallas kernels, local(): pl.pallas_call(unpack, out_shape=(jax.ShapeDtypeStruct((1, lev), f32), ja...  0.7 us

profile of v1, /device:TPU:0, one launch (start us, length us, event | category | flops | bytes accessed | tf_op | source)
XLA Modules:
  0.0 32.5 jit_solution(6714267686152197742)
XLA Ops:
  0.6 31.1 %binned_corr.1.packed = f32[8,128]{1,0:T(8,128)S(1)} custom-call(bf16[80,8,512]{2,1,0:T(8,128)(2,1)} %ens.1, s32[32,128]{1,0:T(8,128)} %bitcast.5, s32[32,128]{1,0:T(8,128)} %bitcast.6, s32[32,128]{1,0:T(8,128)} %bitcast.7), custom_call_target="tpu_custom_call" | custom-call | tf_op jit(solution)/shard_map/binned_corr/pallas_call | solution.py:268
  31.8 0.7 %unpack.1 = (f32[1,8]{1,0:T(1,128)}, f32[8,8]{1,0:T(8,128)}, f32[1,8]{1,0:T(1,128)}) custom-call(f32[8,128]{1,0:T(8,128)S(1)} %binned_corr.1.packed), custom_call_target="tpu_custom_call" | custom-call | tf_op jit(solution)/shard_map/unpack/pallas_call | solution.py:300

commit v2 on v1

v2 whole, which is shorter than its diff:
```python
import functools

import jax
import jax.numpy as jnp
from jax import lax
from jax.experimental import pallas as pl
from jax.experimental.pallas import tpu as pltpu
from jax.sharding import PartitionSpec as P

BIN_DEV = 8
LANES = 128
PAIR_CHUNK = 512
SLOTS = LANES // BIN_DEV
MESH = pl.DeviceIdType.MESH


def pieces3(x):
    a = x.astype(jnp.bfloat16).astype(jnp.float32)
    r = x - a
    b = r.astype(jnp.bfloat16).astype(jnp.float32)
    return a, b, r - b


def onehot(rows, base, count):
    ids = lax.broadcasted_iota(jnp.int32, (count, LANES), 0) + base
    parts = [jnp.where(ids == r, 1.0, 0.0) for r in rows]
    return jnp.concatenate(parts, axis=1).astype(jnp.bfloat16)


def inverse_spread(sq, members):
    inv = 1.0 / jnp.sqrt(sq / (members - 1) + 1e-06)
    hi = inv.astype(jnp.bfloat16).astype(jnp.float32)
    return jnp.concatenate([hi, inv - hi], axis=0).astype(jnp.bfloat16)


def perturb(raw, out, squares, c):
    members, lev = raw.shape[0], raw.shape[1]
    rows = members * lev
    cs = pl.ds(c, LANES)
    x = raw[:, :, cs].astype(jnp.float32)
    mean = jnp.sum(x, axis=0) / members
    pert = (x - mean[None]).astype(jnp.bfloat16).astype(jnp.float32)
    sq = jnp.sum(pert * pert, axis=0)
    out[pl.ds(0, rows), cs] = pert.reshape(rows, LANES).astype(jnp.bfloat16)
    out[pl.ds(rows, 2 * lev), cs] = inverse_spread(sq, members)
    squares[:, cs] = sq


def sum_squares(table, first, last, lev):
    x = table[pl.ds(first, last - first), :].astype(jnp.float32)
    return jnp.sum((x * x).reshape((last - first) // lev, lev, x.shape[1]), axis=0)


def flatten(x, tile, shift):
    first = tile // SLOTS * LANES
    turn = (shift - BIN_DEV * (tile % SLOTS)) % LANES
    rest = turn if turn + BIN_DEV * (x.shape[0] - 1) >= LANES else 0
    y = pltpu.roll(x[:, first:first + LANES], turn - rest, 1, stride=BIN_DEV, stride_axis=0)
    if rest:
        y = pltpu.roll(y, rest, 1)
    slot = lax.broadcasted_iota(jnp.int32, y.shape, 1) // BIN_DEV
    level = lax.broadcasted_iota(jnp.int32, y.shape, 0)
    return jnp.sum(jnp.where(slot == level + shift // BIN_DEV, y, 0.0), axis=0, keepdims=True)


def kernel(
    ntile, nlev, ens, first_in, second_in, bin_in, packed,
    raw, own, halo, lst, plst, squares, right_buf, cov_buf, ia_buf, ib_buf,
    hot_buf, bin_hot, pbin_hot, parts_buf, base_buf, count_buf, sbuf, rbuf,
    load_sem, halo_send, halo_recv, list_send, list_recv, x_send, x_recv, ready,
):
    members, lev, cols = ens.shape
    rows = members * lev
    half = cols // 2
    blocks = cols // LANES
    total_bins, npairs = bin_hot.shape
    chunks = npairs // PAIR_CHUNK
    groups = PAIR_CHUNK // LANES
    cut = members * 3 // 5 // 2 * 2 * lev
    me = lax.axis_index("tile")
    my_lev = lax.axis_index("lev")
    after = lax.rem(me + 1, ntile)

    barrier = pltpu.get_barrier_semaphore()
    for d in range(1, ntile):
        pl.semaphore_signal(
            barrier, inc=1, device_id=(lax.rem(me + d, ntile), my_lev), device_id_type=MESH
        )
    for d in range(1, nlev):
        pl.semaphore_signal(
            barrier, inc=1, device_id=(me, lax.rem(my_lev + d, nlev)), device_id_type=MESH
        )
    loads = [
        pltpu.make_async_copy(
            ens.at[:, :, pl.ds(c * LANES, LANES)], raw.at[:, :, pl.ds(c * LANES, LANES)], load_sem.at[c]
        )
        for c in range(blocks)
    ]
    list_loads = [
        pltpu.make_async_copy(s, lst.at[i], load_sem.at[blocks + i])
        for i, s in enumerate((first_in, second_in, bin_in))
    ]
    for c in loads[:1] + list_loads + loads[1:]:
        c.start()

    share = lst.shape[1] // nlev
    quarter = pl.ds(pl.multiple_of(my_lev * share, share), share)

    def list_copy(d):
        peer = (me, lax.rem(my_lev + d, nlev)) if d else (after, my_lev)
        src = plst if d else lst
        return pltpu.make_async_remote_copy(
            src_ref=src.at[:, quarter, :], dst_ref=plst.at[:, quarter, :],
            send_sem=list_send.at[d], recv_sem=list_recv.at[my_lev],
            device_id=peer, device_id_type=MESH,
        )

    def piece(i, dst, src_rows, src_cols):
        return pltpu.make_async_remote_copy(
            src_ref=own.at[src_rows, src_cols], dst_ref=dst,
            send_sem=halo_send.at[i], recv_sem=halo_recv.at[i],
            device_id=(after, my_lev), device_id_type=MESH,
        )

    near = half // LANES
    halos = [
        piece(c, halo.at[0, pl.ds(0, rows), pl.ds(c * LANES, LANES)], pl.ds(0, rows), pl.ds(c * LANES, LANES))
        for c in range(near)
    ]
    halos.append(piece(near, halo.at[1, pl.ds(0, cut), :], pl.ds(0, cut), pl.ds(half, half)))
    halos.append(piece(near + 1, halo.at[1, pl.ds(cut, rows - cut), :], pl.ds(cut, rows - cut), pl.ds(half, half)))

    loads[0].wait()
    perturb(raw, own, squares, 0)
    for c in list_loads:
        c.wait()
    pl.semaphore_wait(barrier, ntile - 1 + nlev - 1)
    list_copy(0).start()
    halos[0].start()
    for c in range(1, blocks):
        loads[c].wait()
        perturb(raw, own, squares, c * LANES)
        if c < near:
            halos[c].start()
    halos[near].start()
    halos[near + 1].start()
    for d in range(1, nlev):
        pl.semaphore_signal(
            ready, inc=1, device_id=(me, lax.rem(my_lev + d, nlev)), device_id_type=MESH
        )

    def index_rows(ref, i, j):
        return [ref[i, pl.ds(j * groups + g, 1), :] for g in range(groups)]

    def pairs(j):
        return pl.ds(pl.multiple_of(j * PAIR_CHUNK, PAIR_CHUNK), PAIR_CHUNK)

    def product(a, b):
        return jnp.sum((a * b).reshape(a.shape[0] // lev, lev, PAIR_CHUNK), axis=0)

    def two(x):
        return x[:lev] + x[lev:]

    def corr_parts(cov, ia, ib, last):
        corr = cov * ia * ib / (members - 1)
        return jnp.concatenate([*pieces3(corr), jnp.full_like(corr, last)], axis=0).astype(jnp.bfloat16)

    def gather(table, hot):
        return jnp.dot(table, hot, preferred_element_type=jnp.float32)

    def own_step(j, carry):
        x = own[...]
        left = gather(x, onehot(index_rows(lst, 0, j), 0, cols))
        right = gather(x, onehot(index_rows(lst, 1, j), 0, cols))
        parts_buf[:, pairs(j)] = corr_parts(
            product(left[:rows], right[:rows]), two(left[rows:]), two(right[rows:]), 1.0
        )
        bin_hot[:, pairs(j)] = onehot(index_rows(lst, 2, j), 0, total_bins)
        return carry

    lax.fori_loop(0, chunks // 2, own_step, 0)
    list_copy(0).wait_recv()
    for d in range(1, nlev):
        list_copy(d).start()
    lax.fori_loop(chunks // 2, chunks, own_step, 0)

    def bin_dot(parts, hot):
        return lax.dot_general(
            parts, hot, (((1,), (1,)), ((), ())), preferred_element_type=jnp.float32
        )

    def bin_sums(x):
        return x[:lev] + x[lev:2 * lev] + x[2 * lev:3 * lev]

    binned = bin_dot(parts_buf[...], bin_hot[...])
    base_buf[...] = bin_sums(binned)
    counts = binned[3 * lev:]
    lane = lax.broadcasted_iota(jnp.int32, (lev, LANES), 1)
    level = lax.broadcasted_iota(jnp.int32, (lev, LANES), 0)
    level_squares = jnp.sum(
        jnp.where(lane // BIN_DEV == level + SLOTS // 2, jnp.sum(squares[...], axis=1, keepdims=True), 0.0), axis=0, keepdims=True
    )
    for t in range(ntile):
        sbuf[t, 1:2, :] = level_squares
        count_buf[t] = flatten(counts, t, 0)

    for d in range(1, nlev):
        src = lax.rem(my_lev + d, nlev)
        part = plst.at[:, pl.ds(pl.multiple_of(src * share, share), share), :]
        pltpu.make_async_copy(part, part, list_recv.at[src]).wait()

    def cross_step(j, carry):
        oh = onehot([r - cols for r in index_rows(plst, 1, j)], 0, cols)
        right = gather(own[...], oh)
        right_buf[j] = right[:rows]
        ib_buf[j] = two(right[rows:])
        pbin_hot[:, pairs(j)] = onehot(index_rows(plst, 2, j), 0, total_bins)
        hot_buf[:, pairs(j)] = onehot(index_rows(plst, 0, j), half, half)
        return carry

    lax.fori_loop(0, chunks, cross_step, 0)
    pl.semaphore_wait(ready, nlev - 1)

    for c in range(near):
        halos[c].wait_recv()
    halo[0, pl.ds(rows, 2 * lev), :] = inverse_spread(sum_squares(halo.at[0], 0, rows, lev), members)

    def near_step(j, carry):
        left = gather(halo[0], onehot(index_rows(plst, 0, j), 0, half))
        cov_buf[j] = product(left[:rows], right_buf[j])
        ia_buf[j] = two(left[rows:])
        return carry

    lax.fori_loop(0, chunks, near_step, 0)

    halos[near].wait_recv()
    far = sum_squares(halo.at[1], 0, cut, lev)

    def mid_step(j, carry):
        left = gather(halo[1, pl.ds(0, cut), :], hot_buf[:, pairs(j)])
        cov_buf[j] = cov_buf[j] + product(left, right_buf[j, pl.ds(0, cut), :])
        return carry

    lax.fori_loop(0, chunks, mid_step, 0)

    halos[near + 1].wait_recv()
    far = far + sum_squares(halo.at[1], cut, rows, lev)
    halo[1, pl.ds(rows, 2 * lev), :] = inverse_spread(far, members)

    kept = rows - cut

    def far_step(j, total):
        left = gather(halo[1, pl.ds(cut, kept + 2 * lev), :], hot_buf[:, pairs(j)])
        cov = cov_buf[j] + product(left[:kept], right_buf[j, pl.ds(cut, kept), :])
        ia = ia_buf[j] + two(left[kept:])
        return total + bin_dot(corr_parts(cov, ia, ib_buf[j], 0.0), pbin_hot[:, pairs(j)])

    total = lax.fori_loop(0, chunks, far_step, jnp.zeros((4 * lev, total_bins), jnp.float32), unroll=True)
    sums = base_buf[...] + bin_sums(total)
    for t in range(ntile):
        sbuf[t, 0:1, :] = flatten(sums, t, LANES // 2) + count_buf[t]
    mine = my_lev * ntile + me

    def x_copy(d):
        dl, dt = d // ntile, d % ntile
        peer_t = lax.rem(me + dt, ntile)
        peer_l = lax.rem(my_lev + dl, nlev)
        return pltpu.make_async_remote_copy(
            src_ref=sbuf.at[peer_t], dst_ref=rbuf.at[mine],
            send_sem=x_send.at[d], recv_sem=x_recv.at[mine],
            device_id=(peer_t, peer_l), device_id_type=MESH,
        )

    def x_start(d, carry):
        x_copy(d).start()
        return carry

    def x_wait_send(d, carry):
        x_copy(d).wait_send()
        return carry

    def x_wait(d, carry):
        src = lax.rem(my_lev + d // ntile, nlev) * ntile + lax.rem(me + d % ntile, ntile)
        pltpu.make_async_copy(rbuf.at[src], rbuf.at[src], x_recv.at[src]).wait()
        return carry

    everyone = ntile * nlev
    small = everyone <= 64
    lax.fori_loop(1, everyone, x_start, 0, unroll=small)
    rbuf[mine] = sbuf[me]
    for c in halos:
        c.wait_send()
    for d in range(nlev):
        list_copy(d).wait_send()
    lax.fori_loop(1, everyone, x_wait, 0, unroll=small)
    num = jnp.zeros((1, LANES), jnp.float32)
    den = num
    own_lv = num
    own_bc = num
    for v in range(nlev):
        tot = rbuf[v * ntile]
        for t in range(1, ntile):
            tot = tot + rbuf[v * ntile + t]
        sums, lv = tot[0:1], tot[1:2] / ((members - 1) * cols * ntile)
        bc = sums / jnp.maximum(pltpu.roll(sums, LANES // 2, 1), 1.0)
        num = num + lv * bc
        den = den + lv
        own_lv = jnp.where(my_lev == v, lv, own_lv)
        own_bc = jnp.where(my_lev == v, bc, own_bc)

    def by_level(row):
        turn = LANES // 2 - BIN_DEV * (lev - 1)
        return pltpu.roll(jnp.broadcast_to(row, (lev, LANES)), turn, 1, stride=BIN_DEV, stride_axis=0)

    corr = by_level(own_bc)
    for v in range(lev):
        packed[v:v + 1, :] = corr[lev - 1 - v:lev - v]
    diagonal = lane + level == lev - 1
    packed[lev:lev + 1, :] = jnp.sum(jnp.where(diagonal, by_level(own_lv), 0.0), axis=0, keepdims=True)
    packed[lev + 1:lev + 2, :] = jnp.sum(by_level(num), axis=0, keepdims=True) / jnp.sum(
        by_level(den), axis=0, keepdims=True
    )
    lax.fori_loop(1, everyone, x_wait_send, 0, unroll=small)


def unpack(packed, lv_out, corr_out, avg_out):
    lev = corr_out.shape[0]
    corr_out[...] = packed[0:lev, :BIN_DEV]
    lv_out[...] = packed[lev:lev + 1, :lev]
    avg_out[...] = packed[lev + 1:lev + 2, :BIN_DEV]


def local(ntile, nlev, ensemble, pair_first, pair_second, pair_bin):
    members, lev, cols = ensemble.shape
    npairs = pair_first.shape[0]
    rows = members * lev
    half = cols // 2
    pieces = half // LANES + 2
    chunks = npairs // PAIR_CHUNK
    total_bins = -(-BIN_DEV * ntile // LANES) * LANES
    f32, bf16 = jnp.float32, jnp.bfloat16
    idx = [x.reshape(npairs // LANES, LANES) for x in (pair_first, pair_second, pair_bin)]
    vmem = pl.BlockSpec(memory_space=pltpu.VMEM)
    hbm = pl.BlockSpec(memory_space=pl.ANY)
    packed = pl.pallas_call(
        functools.partial(kernel, ntile, nlev),
        out_shape=jax.ShapeDtypeStruct((2 * lev, LANES), f32),
        in_specs=[hbm] * 4,
        out_specs=vmem,
        scratch_shapes=[
            pltpu.VMEM((members, lev, cols), bf16),
            pltpu.VMEM((rows + 2 * lev, cols), bf16),
            pltpu.VMEM((2, rows + 2 * lev, half), bf16),
            pltpu.VMEM((3, npairs // LANES, LANES), jnp.int32),
            pltpu.VMEM((3, npairs // LANES, LANES), jnp.int32),
            pltpu.VMEM((lev, cols), f32),
            pltpu.VMEM((chunks, rows, PAIR_CHUNK), f32),
            *[pltpu.VMEM((chunks, lev, PAIR_CHUNK), f32)] * 3,
            pltpu.VMEM((half, npairs), bf16),
            pltpu.VMEM((total_bins, npairs), bf16),
            pltpu.VMEM((total_bins, npairs), bf16),
            pltpu.VMEM((4 * lev, npairs), bf16),
            pltpu.VMEM((lev, total_bins), f32),
            pltpu.VMEM((ntile, 1, LANES), f32),
            pltpu.VMEM((ntile, 2, LANES), f32),
            pltpu.VMEM((nlev * ntile, 2, LANES), f32),
            pltpu.SemaphoreType.DMA((cols // LANES + 3,)),
            pltpu.SemaphoreType.DMA((pieces,)),
            pltpu.SemaphoreType.DMA((pieces,)),
            pltpu.SemaphoreType.DMA((nlev,)),
            pltpu.SemaphoreType.DMA((nlev,)),
            pltpu.SemaphoreType.DMA((nlev * ntile,)),
            pltpu.SemaphoreType.DMA((nlev * ntile,)),
            pltpu.SemaphoreType.REGULAR,
        ],
        compiler_params=pltpu.CompilerParams(
            collective_id=0, has_side_effects=True, vmem_limit_bytes=55220 * 1024
        ),
        name="binned_corr",
    )(ensemble, *idx)
    lv, corr, avg = pl.pallas_call(
        unpack,
        out_shape=(
            jax.ShapeDtypeStruct((1, lev), f32),
            jax.ShapeDtypeStruct((lev, BIN_DEV), f32),
            jax.ShapeDtypeStruct((1, BIN_DEV), f32),
        ),
        in_specs=[vmem],
        out_specs=(vmem, vmem, vmem),
        compiler_params=pltpu.CompilerParams(vmem_limit_bytes=4 * 1024 * 1024),
        name="unpack",
    )(packed)
    return lv.reshape(lev), corr, avg.reshape(BIN_DEV)


def solution(mesh):
    in_specs = (P(None, "lev", "tile"), P("tile"), P("tile"), P("tile"))
    out_specs = (P("lev"), P("lev", "tile"), P("tile"))
    body = functools.partial(local, mesh.shape["tile"], mesh.shape["lev"])
    return jax.shard_map(body, mesh=mesh, in_specs=in_specs, out_specs=out_specs, check_vma=False)
```

time: 32.6 us -> 31.9 us (0.979)
  Pallas kernels: 31.8 us -> 31.1 us
    pallas_call x1, Pallas kernels: 31.1 us -> 30.5 us  [local(): pl.pallas_call(functools.partial(kernel, ntile, nlev), out_shape=jax.Shap...]
where the time goes in v2:
time: 31.9 us; the launch traced here: 31.8 us
  Pallas kernels  31.1 us (97%)
  between operations  0.64 us (2%)
    pallas_call x1, Pallas kernels, local(): pl.pallas_call(functools.partial(kernel, ntile, nlev), out_shape=jax.Shap...  30.5 us

profile of v2, /device:TPU:0, one launch (start us, length us, event | category | flops | bytes accessed | tf_op | source)
XLA Modules:
  0.0 31.8 jit_solution(354333883960991044)
XLA Ops:
  0.6 30.5 %binned_corr.1.packed = f32[16,128]{1,0:T(8,128)S(1)} custom-call(bf16[80,8,512]{2,1,0:T(8,128)(2,1)} %ens.1, s32[32,128]{1,0:T(8,128)} %bitcast.5, s32[32,128]{1,0:T(8,128)} %bitcast.6, s32[32,128]{1,0:T(8,128)} %bitcast.7), custom_call_target="tpu_custom_call" | custom-call | tf_op jit(solution)/shard_map/binned_corr/pallas_call | solution.py:345
  31.2 0.6 %unpack.1 = (f32[1,8]{1,0:T(1,128)}, f32[8,8]{1,0:T(8,128)}, f32[1,8]{1,0:T(1,128)}) custom-call(f32[16,128]{1,0:T(8,128)S(1)} %binned_corr.1.packed), custom_call_target="tpu_custom_call" | custom-call | tf_op jit(solution)/shard_map/unpack/pallas_call | solution.py:381

commit v3 on v2

--- a/solution.py
+++ b/solution.py
@@ -11,6 +11,8 @@
 LANES = 128
 PAIR_CHUNK = 512
 SLOTS = LANES // BIN_DEV
+OWN, CROSS, NEAR, MID = 2, 4, 8, 8
+CUTS = (12, 16)
 MESH = pl.DeviceIdType.MESH
 
 
@@ -66,7 +68,7 @@
 def kernel(
     ntile, nlev, ens, first_in, second_in, bin_in, packed,
     raw, own, halo, lst, plst, squares, right_buf, cov_buf, ia_buf, ib_buf,
-    hot_buf, bin_hot, pbin_hot, parts_buf, base_buf, count_buf, sbuf, rbuf,
+    bin_hot, parts_buf, base_buf, wide_buf, count_buf, sbuf, rbuf,
     load_sem, halo_send, halo_recv, list_send, list_recv, x_send, x_recv, ready,
 ):
     members, lev, cols = ens.shape
@@ -76,7 +78,7 @@
     total_bins, npairs = bin_hot.shape
     chunks = npairs // PAIR_CHUNK
     groups = PAIR_CHUNK // LANES
-    cut = members * 3 // 5 // 2 * 2 * lev
+    cuts = [0] + [members * n // 20 // 2 * 2 * lev for n in CUTS] + [rows]
     me = lax.axis_index("tile")
     my_lev = lax.axis_index("lev")
     after = lax.rem(me + 1, ntile)
@@ -127,8 +129,9 @@
         piece(c, halo.at[0, pl.ds(0, rows), pl.ds(c * LANES, LANES)], pl.ds(0, rows), pl.ds(c * LANES, LANES))
         for c in range(near)
     ]
-    halos.append(piece(near, halo.at[1, pl.ds(0, cut), :], pl.ds(0, cut), pl.ds(half, half)))
-    halos.append(piece(near + 1, halo.at[1, pl.ds(cut, rows - cut), :], pl.ds(cut, rows - cut), pl.ds(half, half)))
+    spans = list(zip(cuts[:-1], cuts[1:]))
+    for i, (a, b) in enumerate(spans):
+        halos.append(piece(near + i, halo.at[1, pl.ds(a, b - a), :], pl.ds(a, b - a), pl.ds(half, half)))
 
     loads[0].wait()
     perturb(raw, own, squares, 0)
@@ -142,8 +145,8 @@
         perturb(raw, own, squares, c * LANES)
         if c < near:
             halos[c].start()
-    halos[near].start()
-    halos[near + 1].start()
+    for c in halos[near:]:
+        c.start()
     for d in range(1, nlev):
         pl.semaphore_signal(
             ready, inc=1, device_id=(me, lax.rem(my_lev + d, nlev)), device_id_type=MESH
@@ -178,11 +181,11 @@
         bin_hot[:, pairs(j)] = onehot(index_rows(lst, 2, j), 0, total_bins)
         return carry
 
-    lax.fori_loop(0, chunks // 2, own_step, 0)
+    lax.fori_loop(0, chunks // 2, own_step, 0, unroll=OWN)
     list_copy(0).wait_recv()
     for d in range(1, nlev):
         list_copy(d).start()
-    lax.fori_loop(chunks // 2, chunks, own_step, 0)
+    lax.fori_loop(chunks // 2, chunks, own_step, 0, unroll=OWN)
 
     def bin_dot(parts, hot):
         return lax.dot_general(
@@ -194,7 +197,9 @@
 
     binned = bin_dot(parts_buf[...], bin_hot[...])
     base_buf[...] = bin_sums(binned)
-    counts = binned[3 * lev:]
+    wide_buf[...] = jnp.zeros_like(wide_buf)
+    wide_buf[0, :, pl.ds(0, total_bins)] = binned[3 * lev:]
+    counts = wide_buf[0]
     lane = lax.broadcasted_iota(jnp.int32, (lev, LANES), 1)
     level = lax.broadcasted_iota(jnp.int32, (lev, LANES), 0)
     level_squares = jnp.sum(
@@ -214,11 +219,9 @@
         right = gather(own[...], oh)
         right_buf[j] = right[:rows]
         ib_buf[j] = two(right[rows:])
-        pbin_hot[:, pairs(j)] = onehot(index_rows(plst, 2, j), 0, total_bins)
-        hot_buf[:, pairs(j)] = onehot(index_rows(plst, 0, j), half, half)
         return carry
 
-    lax.fori_loop(0, chunks, cross_step, 0)
+    lax.fori_loop(0, chunks, cross_step, 0, unroll=CROSS)
     pl.semaphore_wait(ready, nlev - 1)
 
     for c in range(near):
@@ -231,58 +234,54 @@
         ia_buf[j] = two(left[rows:])
         return carry
 
-    lax.fori_loop(0, chunks, near_step, 0)
-
-    halos[near].wait_recv()
-    far = sum_squares(halo.at[1], 0, cut, lev)
-
-    def mid_step(j, carry):
-        left = gather(halo[1, pl.ds(0, cut), :], hot_buf[:, pairs(j)])
-        cov_buf[j] = cov_buf[j] + product(left, right_buf[j, pl.ds(0, cut), :])
-        return carry
-
-    lax.fori_loop(0, chunks, mid_step, 0)
-
-    halos[near + 1].wait_recv()
+    lax.fori_loop(0, chunks, near_step, 0, unroll=NEAR)
+
+    far = jnp.zeros((lev, half), jnp.float32)
+    for i, (a, b) in enumerate(spans[:-1]):
+        halos[near + i].wait_recv()
+        far = far + sum_squares(halo.at[1], a, b, lev)
+
+        def mid_step(j, carry):
+            left = gather(halo[1, pl.ds(a, b - a), :], onehot(index_rows(plst, 0, j), half, half))
+            cov_buf[j] = cov_buf[j] + product(left, right_buf[j, pl.ds(a, b - a), :])
+            return carry
+
+        lax.fori_loop(0, chunks, mid_step, 0, unroll=MID)
+
+    cut = cuts[-2]
+    halos[-1].wait_recv()
     far = far + sum_squares(halo.at[1], cut, rows, lev)
     halo[1, pl.ds(rows, 2 * lev), :] = inverse_spread(far, members)
 
     kept = rows - cut
 
     def far_step(j, total):
-        left = gather(halo[1, pl.ds(cut, kept + 2 * lev), :], hot_buf[:, pairs(j)])
+        left = gather(halo[1, pl.ds(cut, kept + 2 * lev), :], onehot(index_rows(plst, 0, j), half, half))
         cov = cov_buf[j] + product(left[:kept], right_buf[j, pl.ds(cut, kept), :])
         ia = ia_buf[j] + two(left[kept:])
-        return total + bin_dot(corr_parts(cov, ia, ib_buf[j], 0.0), pbin_hot[:, pairs(j)])
+        return total + bin_dot(corr_parts(cov, ia, ib_buf[j], 0.0), onehot(index_rows(plst, 2, j), 0, total_bins))
 
     total = lax.fori_loop(0, chunks, far_step, jnp.zeros((4 * lev, total_bins), jnp.float32), unroll=True)
-    sums = base_buf[...] + bin_sums(total)
+    wide_buf[1, :, pl.ds(0, total_bins)] = base_buf[...] + bin_sums(total)
+    sums = wide_buf[1]
     for t in range(ntile):
         sbuf[t, 0:1, :] = flatten(sums, t, LANES // 2) + count_buf[t]
     mine = my_lev * ntile + me
 
-    def x_copy(d):
+    def x_start(d, carry):
         dl, dt = d // ntile, d % ntile
         peer_t = lax.rem(me + dt, ntile)
         peer_l = lax.rem(my_lev + dl, nlev)
-        return pltpu.make_async_remote_copy(
+        pltpu.make_async_remote_copy(
             src_ref=sbuf.at[peer_t], dst_ref=rbuf.at[mine],
-            send_sem=x_send.at[d], recv_sem=x_recv.at[mine],
+            send_sem=x_send.at[0], recv_sem=x_recv.at[0],
             device_id=(peer_t, peer_l), device_id_type=MESH,
-        )
-
-    def x_start(d, carry):
-        x_copy(d).start()
+        ).start()
         return carry
 
-    def x_wait_send(d, carry):
-        x_copy(d).wait_send()
-        return carry
-
-    def x_wait(d, carry):
-        src = lax.rem(my_lev + d // ntile, nlev) * ntile + lax.rem(me + d % ntile, ntile)
-        pltpu.make_async_copy(rbuf.at[src], rbuf.at[src], x_recv.at[src]).wait()
-        return carry
+    def x_wait(sem):
+        rest = rbuf.at[pl.ds(0, everyone - 1)]
+        pltpu.make_async_copy(rest, rest, sem).wait()
 
     everyone = ntile * nlev
     small = everyone <= 64
@@ -292,7 +291,8 @@
         c.wait_send()
     for d in range(nlev):
         list_copy(d).wait_send()
-    lax.fori_loop(1, everyone, x_wait, 0, unroll=small)
+    x_wait(x_send.at[0])
+    x_wait(x_recv.at[0])
     num = jnp.zeros((1, LANES), jnp.float32)
     den = num
     own_lv = num
@@ -320,7 +320,6 @@
     packed[lev + 1:lev + 2, :] = jnp.sum(by_level(num), axis=0, keepdims=True) / jnp.sum(
         by_level(den), axis=0, keepdims=True
     )
-    lax.fori_loop(1, everyone, x_wait_send, 0, unroll=small)
 
 
 def unpack(packed, lv_out, corr_out, avg_out):
@@ -335,9 +334,10 @@
     npairs = pair_first.shape[0]
     rows = members * lev
     half = cols // 2
-    pieces = half // LANES + 2
+    pieces = half // LANES + len(CUTS) + 1
     chunks = npairs // PAIR_CHUNK
-    total_bins = -(-BIN_DEV * ntile // LANES) * LANES
+    total_bins = BIN_DEV * ntile
+    bin_lanes = -(-total_bins // LANES) * LANES
     f32, bf16 = jnp.float32, jnp.bfloat16
     idx = [x.reshape(npairs // LANES, LANES) for x in (pair_first, pair_second, pair_bin)]
     vmem = pl.BlockSpec(memory_space=pltpu.VMEM)
@@ -356,11 +356,10 @@
             pltpu.VMEM((lev, cols), f32),
             pltpu.VMEM((chunks, rows, PAIR_CHUNK), f32),
             *[pltpu.VMEM((chunks, lev, PAIR_CHUNK), f32)] * 3,
-            pltpu.VMEM((half, npairs), bf16),
-            pltpu.VMEM((total_bins, npairs), bf16),
             pltpu.VMEM((total_bins, npairs), bf16),
             pltpu.VMEM((4 * lev, npairs), bf16),
             pltpu.VMEM((lev, total_bins), f32),
+            pltpu.VMEM((2, lev, bin_lanes), f32),
             pltpu.VMEM((ntile, 1, LANES), f32),
             pltpu.VMEM((ntile, 2, LANES), f32),
             pltpu.VMEM((nlev * ntile, 2, LANES), f32),
@@ -369,8 +368,8 @@
             pltpu.SemaphoreType.DMA((pieces,)),
             pltpu.SemaphoreType.DMA((nlev,)),
             pltpu.SemaphoreType.DMA((nlev,)),
-            pltpu.SemaphoreType.DMA((nlev * ntile,)),
-            pltpu.SemaphoreType.DMA((nlev * ntile,)),
+            pltpu.SemaphoreType.DMA((1,)),
+            pltpu.SemaphoreType.DMA((1,)),
             pltpu.SemaphoreType.REGULAR,
         ],
         compiler_params=pltpu.CompilerParams(

time: 31.9 us -> 28.5 us (0.89)
  Pallas kernels: 31.1 us -> 27.7 us
    pallas_call x1, Pallas kernels: 30.5 us -> 27.1 us  [local(): pl.pallas_call(functools.partial(kernel, ntile, nlev), out_shape=jax.Shap...]
where the time goes in v3:
time: 28.5 us; the launch traced here: 28.3 us
  Pallas kernels  27.7 us (97%)
  between operations  0.64 us (2%)
    pallas_call x1, Pallas kernels, local(): pl.pallas_call(functools.partial(kernel, ntile, nlev), out_shape=jax.Shap...  27.1 us
    pallas_call x1, Pallas kernels, local(): pl.pallas_call(unpack, out_shape=(jax.ShapeDtypeStruct((1, lev), f32), ja...  0.6 us

profile of v3, /device:TPU:0, one launch (start us, length us, event | category | flops | bytes accessed | tf_op | source)
XLA Modules:
  0.0 28.3 jit_solution(15731761466087384802)
XLA Ops:
  0.6 27.1 %binned_corr.1.packed = f32[16,128]{1,0:T(8,128)S(1)} custom-call(bf16[80,8,512]{2,1,0:T(8,128)(2,1)} %ens.1, s32[32,128]{1,0:T(8,128)} %bitcast.5, s32[32,128]{1,0:T(8,128)} %bitcast.6, s32[32,128]{1,0:T(8,128)} %bitcast.7), custom_call_target="tpu_custom_call" | custom-call | tf_op jit(solution)/shard_map/binned_corr/pallas_call | solution.py:345
  27.7 0.6 %unpack.1 = (f32[1,8]{1,0:T(1,128)}, f32[8,8]{1,0:T(8,128)}, f32[1,8]{1,0:T(1,128)}) custom-call(f32[16,128]{1,0:T(8,128)S(1)} %binned_corr.1.packed), custom_call_target="tpu_custom_call" | custom-call | tf_op jit(solution)/shard_map/unpack/pallas_call | solution.py:380

commit v4 on v3

v4 whole, which is shorter than its diff:
```python
import functools

import jax
import jax.numpy as jnp
from jax import lax
from jax.experimental import pallas as pl
from jax.experimental.pallas import tpu as pltpu
from jax.sharding import PartitionSpec as P

BIN_DEV = 8
LANES = 128
PAIR_CHUNK = 512
SLOTS = LANES // BIN_DEV
OWN, CROSS, NEAR = 2, 4, 8
HOT = jnp.float8_e4m3fn
CUTS = (12, 16)
MESH = pl.DeviceIdType.MESH


def onehot(rows, base, count):
    ids = lax.broadcasted_iota(jnp.int32, (count, LANES), 0) + base
    parts = [jnp.where(ids == r, 1.0, 0.0) for r in rows]
    return jnp.concatenate(parts, axis=1).astype(jnp.bfloat16)


def inverse_spread(sq, members):
    inv = 1.0 / jnp.sqrt(sq / (members - 1) + 1e-06)
    hi = inv.astype(jnp.bfloat16).astype(jnp.float32)
    return jnp.concatenate([hi, inv - hi], axis=0).astype(jnp.bfloat16)


def perturb(raw, out, squares, c):
    members, lev = raw.shape[0], raw.shape[1]
    rows = members * lev
    cs = pl.ds(c, LANES)
    x = raw[:, :, cs].astype(jnp.float32)
    mean = jnp.sum(x, axis=0) / members
    pert = (x - mean[None]).astype(jnp.bfloat16).astype(jnp.float32)
    sq = jnp.sum(pert * pert, axis=0)
    out[pl.ds(0, rows), cs] = pert.reshape(rows, LANES).astype(jnp.bfloat16)
    out[pl.ds(rows, 2 * lev), cs] = inverse_spread(sq, members)
    squares[:, cs] = sq


def sum_squares(table, first, last, col, count, lev):
    x = table[pl.ds(first, last - first), pl.ds(col, count)].astype(jnp.float32)
    return jnp.sum((x * x).reshape((last - first) // lev, lev, x.shape[1]), axis=0)


def flatten(x, tile, shift):
    first = tile // SLOTS * LANES
    turn = (shift - BIN_DEV * (tile % SLOTS)) % LANES
    rest = turn if turn + BIN_DEV * (x.shape[0] - 1) >= LANES else 0
    y = pltpu.roll(x[:, first:first + LANES], turn - rest, 1, stride=BIN_DEV, stride_axis=0)
    if rest:
        y = pltpu.roll(y, rest, 1)
    slot = lax.broadcasted_iota(jnp.int32, y.shape, 1) // BIN_DEV
    level = lax.broadcasted_iota(jnp.int32, y.shape, 0)
    return jnp.sum(jnp.where(slot == level + shift // BIN_DEV, y, 0.0), axis=0, keepdims=True)


def kernel(
    ntile, nlev, ens, first_in, second_in, bin_in, packed,
    raw, own, halo, lst, pack, plst, squares, right_buf, cov_buf, ia_buf, ib_buf,
    hot_buf, bin_hot, pbin_hot, parts_buf, base_buf, wide_buf, early_out, early_in, variance, scale, sbuf, rbuf,
    load_sem, halo_send, halo_recv, list_sem, early_sem, x_sem, ready,
):
    members, lev, cols = ens.shape
    rows = members * lev
    half = cols // 2
    blocks = cols // LANES
    total_bins, npairs = bin_hot.shape
    chunks = npairs // PAIR_CHUNK
    groups = PAIR_CHUNK // LANES
    cuts = [0] + [members * n // 20 // 2 * 2 * lev for n in CUTS] + [rows]
    me = lax.axis_index("tile")
    my_lev = lax.axis_index("lev")
    after = lax.rem(me + 1, ntile)

    barrier = pltpu.get_barrier_semaphore()
    for d in range(1, ntile):
        pl.semaphore_signal(
            barrier, inc=1, device_id=(lax.rem(me + d, ntile), my_lev), device_id_type=MESH
        )
    for d in range(1, nlev):
        pl.semaphore_signal(
            barrier, inc=1, device_id=(me, lax.rem(my_lev + d, nlev)), device_id_type=MESH
        )
    loads = [
        pltpu.make_async_copy(
            ens.at[:, :, pl.ds(c * LANES, LANES)], raw.at[:, :, pl.ds(c * LANES, LANES)], load_sem.at[c]
        )
        for c in range(blocks)
    ]
    list_loads = [
        pltpu.make_async_copy(s, lst.at[i], load_sem.at[blocks])
        for i, s in enumerate((first_in, second_in, bin_in))
    ]
    for c in loads[:1] + list_loads + loads[1:]:
        c.start()

    share = lst.shape[1] // nlev
    quarter = pl.ds(pl.multiple_of(my_lev * share, share), share)

    def list_copy(d):
        peer = (me, lax.rem(my_lev + d, nlev)) if d else (after, my_lev)
        src = plst if d else pack
        return pltpu.make_async_remote_copy(
            src_ref=src.at[:, quarter, :], dst_ref=plst.at[:, quarter, :],
            send_sem=list_sem.at[0], recv_sem=list_sem.at[2 if d else 1],
            device_id=peer, device_id_type=MESH,
        )

    def piece(i, dst, src_rows, src_cols):
        return pltpu.make_async_remote_copy(
            src_ref=own.at[src_rows, src_cols], dst_ref=dst,
            send_sem=halo_send.at[0], recv_sem=halo_recv.at[i],
            device_id=(after, my_lev), device_id_type=MESH,
        )

    near = half // LANES
    halos = [
        piece(c, halo.at[0, pl.ds(0, rows), pl.ds(c * LANES, LANES)], pl.ds(0, rows), pl.ds(c * LANES, LANES))
        for c in range(near)
    ]
    spans = [(a, b, 0, half) for a, b in zip(cuts[:-2], cuts[1:-1])]
    cut = cuts[-2]
    spans += [(cut, rows, 0, half)]
    for i, (a, b, c, n) in enumerate(spans):
        r = pl.ds(a, b - a)
        halos.append(piece(near + i, halo.at[1, r, pl.ds(c, n)], r, pl.ds(half + c, n)))

    loads[0].wait()
    perturb(raw, own, squares, 0)
    pltpu.make_async_copy(lst, lst, load_sem.at[blocks]).wait()
    pack[0] = lst[0] + lst[1] * 65536
    pack[1] = lst[2]
    pl.semaphore_wait(barrier, ntile - 1 + nlev - 1)
    list_copy(0).start()
    halos[0].start()
    for c in range(1, blocks):
        loads[c].wait()
        perturb(raw, own, squares, c * LANES)
        if c < near:
            halos[c].start()
    for d in range(1, nlev):
        pl.semaphore_signal(
            ready, inc=1, device_id=(me, lax.rem(my_lev + d, nlev)), device_id_type=MESH
        )

    def index_rows(ref, i, j):
        return [ref[i, pl.ds(j * groups + g, 1), :] for g in range(groups)]

    def first_rows(j):
        return [r & 65535 for r in index_rows(plst, 0, j)]

    def pairs(j):
        return pl.ds(pl.multiple_of(j * PAIR_CHUNK, PAIR_CHUNK), PAIR_CHUNK)

    def product(a, b):
        return jnp.sum((a * b).reshape(a.shape[0] // lev, lev, PAIR_CHUNK), axis=0)

    def two(x):
        return x[:lev] + x[lev:]

    def corr_parts(cov, ia, ib):
        corr = cov * ia * ib
        hi = corr.astype(jnp.bfloat16).astype(jnp.float32)
        return jnp.concatenate([hi, corr - hi], axis=0).astype(jnp.bfloat16)

    def gather(table, hot):
        return jnp.dot(table, hot, preferred_element_type=jnp.float32)

    def bin_dot(parts, hot):
        return lax.dot_general(
            parts, hot, (((1,), (1,)), ((), ())), preferred_element_type=jnp.float32
        )

    def bin_step(j, carry):
        bin_hot[:, pairs(j)] = onehot(index_rows(lst, 2, j), 0, total_bins)
        return carry

    wide_buf[...] = jnp.zeros_like(wide_buf)
    lax.fori_loop(0, chunks, bin_step, 0)
    ones = jnp.ones((2 * lev, npairs), jnp.bfloat16)
    wide_buf[0, :, pl.ds(0, total_bins)] = bin_dot(ones, bin_hot[...])[:lev]
    counts = wide_buf[0]
    lane = lax.broadcasted_iota(jnp.int32, (lev, LANES), 1)
    level = lax.broadcasted_iota(jnp.int32, (lev, LANES), 0)
    level_squares = jnp.sum(
        jnp.where(lane // BIN_DEV == level + SLOTS // 2, jnp.sum(squares[...], axis=1, keepdims=True), 0.0), axis=0, keepdims=True
    )
    for t in range(ntile):
        early_out[t, 0:1, :] = flatten(counts, t, LANES // 2)
        early_out[t, 1:2, :] = level_squares
    early_in[me] = early_out[me]

    def early_start(d, carry):
        peer = lax.rem(me + d, ntile)
        pltpu.make_async_remote_copy(
            src_ref=early_out.at[peer], dst_ref=early_in.at[me],
            send_sem=early_sem.at[0], recv_sem=early_sem.at[1],
            device_id=(peer, my_lev), device_id_type=MESH,
        ).start()
        return carry

    lax.fori_loop(1, ntile, early_start, 0, unroll=ntile <= 16)

    def wait_all(ref, count, sem):
        part = ref.at[pl.ds(0, count)]
        pltpu.make_async_copy(part, part, sem).wait()


    for c in halos[near:]:
        c.start()

    def own_step(j, carry):
        x = own[...]
        left = gather(x, onehot(index_rows(lst, 0, j), 0, cols))
        right = gather(x, onehot(index_rows(lst, 1, j), 0, cols))
        parts_buf[:, pairs(j)] = corr_parts(
            product(left[:rows], right[:rows]), two(left[rows:]), two(right[rows:]) / (members - 1)
        )
        return carry

    lax.fori_loop(0, chunks // 2, own_step, 0, unroll=OWN)
    list_copy(0).wait_recv()
    for d in range(1, nlev):
        list_copy(d).start()
    lax.fori_loop(chunks // 2, chunks, own_step, 0, unroll=OWN)

    binned = bin_dot(parts_buf[...], bin_hot[...])
    base_buf[...] = two(binned)
    part = plst.at[:, pl.ds(0, (nlev - 1) * share), :]
    pltpu.make_async_copy(part, part, list_sem.at[2]).wait()

    def cross_step(j, carry):
        oh = onehot([(r >> 16) - cols for r in index_rows(plst, 0, j)], 0, cols)
        right = gather(own[...], oh)
        right_buf[j] = right[:rows]
        ib_buf[j] = two(right[rows:]) / (members - 1)
        hot_buf[:, pairs(j)] = onehot(first_rows(j), half, half).astype(HOT)
        pbin_hot[:, pairs(j)] = onehot(index_rows(plst, 1, j), 0, total_bins).astype(HOT)
        return carry

    lax.fori_loop(0, chunks, cross_step, 0, unroll=CROSS)
    pl.semaphore_wait(ready, nlev - 1)

    for c in range(near):
        halos[c].wait_recv()
    halo[0, pl.ds(rows, 2 * lev), :] = inverse_spread(sum_squares(halo.at[0], 0, rows, 0, half, lev), members)

    def near_step(j, carry):
        left = gather(halo[0], onehot(first_rows(j), 0, half))
        cov_buf[j] = product(left[:rows], right_buf[j])
        ia_buf[j] = two(left[rows:])
        return carry

    lax.fori_loop(0, chunks, near_step, 0, unroll=NEAR)
    wait_all(early_in, ntile - 1, early_sem.at[0])
    wait_all(early_in, ntile - 1, early_sem.at[1])
    early = early_in[0]
    for t in range(1, ntile):
        early = early + early_in[t]
    scale[0:1, :] = 1.0 / jnp.maximum(early[0:1], 1.0)
    variance[my_lev] = early[1:2] / ((members - 1) * cols * ntile)
    lev_copies = [
        pltpu.make_async_remote_copy(
            src_ref=variance.at[my_lev], dst_ref=variance.at[my_lev],
            send_sem=early_sem.at[2], recv_sem=early_sem.at[3],
            device_id=(me, lax.rem(my_lev + d, nlev)), device_id_type=MESH,
        )
        for d in range(1, nlev)
    ]
    for c in lev_copies:
        c.start()

    def by_level(row):
        turn = LANES // 2 - BIN_DEV * (lev - 1)
        return pltpu.roll(jnp.broadcast_to(row, (lev, LANES)), turn, 1, stride=BIN_DEV, stride_axis=0)

    far = jnp.zeros((lev, half), jnp.float32)
    kept = rows - cut
    for i, (a, b, c, n) in enumerate(spans):
        halos[near + i].wait_recv()
        sq = sum_squares(halo.at[1], a, b, c, n, lev)
        last = i == len(spans) - 1
        if a < cut:
            far = far + sq
            more = 0
        else:
            halo[1, pl.ds(rows, 2 * lev), pl.ds(c, n)] = inverse_spread(far[:, c:c + n] + sq, members)
            more = 2 * lev

        def far_step(j, acc):
            left = gather(
                halo[1, pl.ds(a, b - a + more), pl.ds(c, n)], hot_buf[pl.ds(c, n), pairs(j)]
            )
            cov = cov_buf[j] + product(left[:b - a], right_buf[j, pl.ds(a, b - a), :])
            ia = ia_buf[j] + two(left[b - a:]) if more else None
            if last:
                parts_buf[:, pairs(j)] = corr_parts(cov, ia, ib_buf[j])
                return acc
            cov_buf[j] = cov
            if more:
                ia_buf[j] = ia
            return acc

        lax.fori_loop(0, chunks, far_step, 0, unroll=True)
        if i == 0:
            wait_all(variance, nlev - 1, early_sem.at[2])
            wait_all(variance, nlev - 1, early_sem.at[3])
        diagonal = lane + level == lev - 1
        packed[lev:lev + 1, :] = jnp.sum(jnp.where(diagonal, by_level(variance[my_lev]), 0.0), axis=0, keepdims=True)
        den = variance[0]
        for v in range(1, nlev):
            den = den + variance[v]
        scale[1:2, :] = 1.0 / jnp.sum(by_level(den), axis=0, keepdims=True)
    wide_buf[1, :, pl.ds(0, total_bins)] = base_buf[...] + two(bin_dot(parts_buf[...], pbin_hot[...]))
    sums = wide_buf[1]
    for t in range(ntile):
        sbuf[t] = flatten(sums, t, LANES // 2)
    mine = my_lev * ntile + me

    def x_start(d, carry):
        dl, dt = d // ntile, d % ntile
        peer_t = lax.rem(me + dt, ntile)
        peer_l = lax.rem(my_lev + dl, nlev)
        pltpu.make_async_remote_copy(
            src_ref=sbuf.at[peer_t], dst_ref=rbuf.at[mine],
            send_sem=x_sem.at[0], recv_sem=x_sem.at[1],
            device_id=(peer_t, peer_l), device_id_type=MESH,
        ).start()
        return carry

    everyone = ntile * nlev
    small = everyone <= 64
    lax.fori_loop(1, everyone, x_start, 0, unroll=small)
    rbuf[mine] = sbuf[me]
    part = own.at[pl.ds(0, rows), :]
    pltpu.make_async_copy(part, part, halo_send.at[0]).wait()
    pltpu.make_async_copy(plst, plst, list_sem.at[0]).wait()
    wait_all(rbuf, everyone - 1, x_sem.at[0])
    wait_all(rbuf, everyone - 1, x_sem.at[1])
    num = jnp.zeros((1, LANES), jnp.float32)
    own_bc = num
    for v in range(nlev):
        tot = rbuf[v * ntile]
        for t in range(1, ntile):
            tot = tot + rbuf[v * ntile + t]
        bc = tot * scale[0:1, :]
        num = num + variance[v] * bc
        own_bc = jnp.where(my_lev == v, bc, own_bc)
    corr = by_level(own_bc)
    for v in range(lev):
        packed[v:v + 1, :] = corr[lev - 1 - v:lev - v]
    packed[lev + 1:lev + 2, :] = jnp.sum(by_level(num), axis=0, keepdims=True) * scale[1:2, :]


def unpack(packed, lv_out, corr_out, avg_out):
    lev = corr_out.shape[0]
    corr_out[...] = packed[0:lev, :BIN_DEV]
    lv_out[...] = packed[lev:lev + 1, :lev]
    avg_out[...] = packed[lev + 1:lev + 2, :BIN_DEV]


def local(ntile, nlev, ensemble, pair_first, pair_second, pair_bin):
    members, lev, cols = ensemble.shape
    npairs = pair_first.shape[0]
    rows = members * lev
    half = cols // 2
    pieces = half // LANES + len(CUTS) + 1
    chunks = npairs // PAIR_CHUNK
    total_bins = BIN_DEV * ntile
    bin_lanes = -(-total_bins // LANES) * LANES
    f32, bf16 = jnp.float32, jnp.bfloat16
    idx = [x.reshape(npairs // LANES, LANES) for x in (pair_first, pair_second, pair_bin)]
    vmem = pl.BlockSpec(memory_space=pltpu.VMEM)
    hbm = pl.BlockSpec(memory_space=pl.ANY)
    packed = pl.pallas_call(
        functools.partial(kernel, ntile, nlev),
        out_shape=jax.ShapeDtypeStruct((2 * lev, LANES), f32),
        in_specs=[hbm] * 4,
        out_specs=vmem,
        scratch_shapes=[
            pltpu.VMEM((members, lev, cols), bf16),
            pltpu.VMEM((rows + 2 * lev, cols), bf16),
            pltpu.VMEM((2, rows + 2 * lev, half), bf16),
            pltpu.VMEM((3, npairs // LANES, LANES), jnp.int32),
            *[pltpu.VMEM((2, npairs // LANES, LANES), jnp.int32)] * 2,
            pltpu.VMEM((lev, cols), f32),
            pltpu.VMEM((chunks, rows, PAIR_CHUNK), f32),
            *[pltpu.VMEM((chunks, lev, PAIR_CHUNK), f32)] * 3,
            pltpu.VMEM((half, npairs), HOT),
            pltpu.VMEM((total_bins, npairs), bf16),
            pltpu.VMEM((total_bins, npairs), HOT),
            pltpu.VMEM((2 * lev, npairs), bf16),
            pltpu.VMEM((lev, total_bins), f32),
            pltpu.VMEM((2, lev, bin_lanes), f32),
            *[pltpu.VMEM((ntile, 2, LANES), f32)] * 2,
            pltpu.VMEM((nlev, 1, LANES), f32),
            pltpu.VMEM((2, LANES), f32),
            pltpu.VMEM((ntile, 1, LANES), f32),
            pltpu.VMEM((nlev * ntile, 1, LANES), f32),
            pltpu.SemaphoreType.DMA((cols // LANES + 1,)),
            pltpu.SemaphoreType.DMA((1,)),
            pltpu.SemaphoreType.DMA((pieces,)),
            pltpu.SemaphoreType.DMA((3,)),
            pltpu.SemaphoreType.DMA((4,)),
            pltpu.SemaphoreType.DMA((2,)),
            pltpu.SemaphoreType.REGULAR,
        ],
        compiler_params=pltpu.CompilerParams(
            collective_id=0, has_side_effects=True, vmem_limit_bytes=55220 * 1024
        ),
        name="binned_corr",
    )(ensemble, *idx)
    lv, corr, avg = pl.pallas_call(
        unpack,
        out_shape=(
            jax.ShapeDtypeStruct((1, lev), f32),
            jax.ShapeDtypeStruct((lev, BIN_DEV), f32),
            jax.ShapeDtypeStruct((1, BIN_DEV), f32),
        ),
        in_specs=[vmem],
        out_specs=(vmem, vmem, vmem),
        compiler_params=pltpu.CompilerParams(vmem_limit_bytes=4 * 1024 * 1024),
        name="unpack",
    )(packed)
    return lv.reshape(lev), corr, avg.reshape(BIN_DEV)


def solution(mesh):
    in_specs = (P(None, "lev", "tile"), P("tile"), P("tile"), P("tile"))
    out_specs = (P("lev"), P("lev", "tile"), P("tile"))
    body = functools.partial(local, mesh.shape["tile"], mesh.shape["lev"])
    return jax.shard_map(body, mesh=mesh, in_specs=in_specs, out_specs=out_specs, check_vma=False)
```

time: 28.5 us -> 28.2 us (0.989)
  Pallas kernels: 27.7 us -> 27.4 us
    pallas_call x1, Pallas kernels: 27.1 us -> 26.8 us  [local(): pl.pallas_call(functools.partial(kernel, ntile, nlev), out_shape=jax.Shap...]
where the time goes in v4:
time: 28.2 us; the launch traced here: 28 us
  Pallas kernels  27.4 us (97%)
  between operations  0.64 us (2%)
    pallas_call x1, Pallas kernels, local(): pl.pallas_call(functools.partial(kernel, ntile, nlev), out_shape=jax.Shap...  26.8 us
    pallas_call x1, Pallas kernels, local(): pl.pallas_call(unpack, out_shape=(jax.ShapeDtypeStruct((1, lev), f32), ja...  0.6 us

profile of v4, /device:TPU:0, one launch (start us, length us, event | category | flops | bytes accessed | tf_op | source)
XLA Modules:
  0.0 28.0 jit_solution(3100420381792622477)
XLA Ops:
  0.6 26.8 %binned_corr.1.packed = f32[16,128]{1,0:T(8,128)S(1)} custom-call(bf16[80,8,512]{2,1,0:T(8,128)(2,1)} %ens.1, s32[32,128]{1,0:T(8,128)} %bitcast.5, s32[32,128]{1,0:T(8,128)} %bitcast.6, s32[32,128]{1,0:T(8,128)} %bitcast.7), custom_call_target="tpu_custom_call" | custom-call | tf_op jit(solution)/shard_map/binned_corr/pallas_call | solution.py:380
  27.4 0.6 %unpack.1 = (f32[1,8]{1,0:T(1,128)}, f32[8,8]{1,0:T(8,128)}, f32[1,8]{1,0:T(1,128)}) custom-call(f32[16,128]{1,0:T(8,128)S(1)} %binned_corr.1.packed), custom_call_target="tpu_custom_call" | custom-call | tf_op jit(solution)/shard_map/unpack/pallas_call | solution.py:418
